TPU v7x, 32 devices: a whole 2x2x4 slice. The times are simulated.
32 devices in a mesh: rows: 4 (over z), snaps: 8 (over y, x, core).
Axes of the slice: x: 2, y: 2, z: 4, core: 2. Of those that a mesh axis runs over, the one named last changes fastest.
Arguments:
- snapshots: float32 [8192, 2048], P('rows', 'snaps'), may hold values from -6 to 6
- weights: float32 [8192], P('rows'), may hold values from 0.3 to 3
- next_bricks: float32 [8192, 2048], P(('rows', 'snaps')), may hold values from -6 to 6
- brick_source: int32 [4, 64], P('rows'), may hold values from 0 to 63, each once within a row
Outputs:
- gram: float32 [2048, 2048], P('rows', 'snaps')
- next_tiles: float32 [8192, 2048], P('rows', 'snaps')
Inputs may be any that keep to these rules, and one draw needn't show every extreme that they name: Each row of brick_source is a permutation of 0 to 63.
All inputs are finite; a program needn't handle non-finite values.
Results may differ from a plain program's by a relative error of at most 0.00007.
Values sent between devices are 32-bit elements; how exact they have to be, the bound alone decides.
A program may use at most 128 MiB of HBM per device.

v0:
```python
import math

import jax
import jax.numpy as jnp
from jax import lax
from jax.sharding import PartitionSpec as P

BRICK = 32


def pair_tile(left, right):
    return lax.dot_general(
        left,
        right,
        (((0,), (0,)), ((), ())),
        precision=lax.Precision.HIGHEST,
        preferred_element_type=jnp.float32,
    )


def per_device(snapshots, weights, next_bricks, brick_source):
    width = snapshots.shape[1]
    rows_here = snapshots.shape[0]
    weighted = snapshots * weights[:, None]
    scale = jnp.float32(math.sqrt(rows_here * lax.axis_size("rows")))
    column = pair_tile(lax.all_gather(snapshots, "snaps", axis=1, tiled=True), weighted)
    arrived = lax.all_to_all(next_bricks, "snaps", split_axis=1, concat_axis=0, tiled=True)
    bricks = arrived.reshape(-1, BRICK, width)
    next_tiles = jnp.take(bricks, brick_source[0], axis=0).reshape(-1, width)
    summed = lax.psum_scatter(column, "rows", scatter_dimension=0, tiled=True)
    return (summed / scale, next_tiles)


def solution(mesh):
    placed = (P("rows", "snaps"), P("rows"), P(("rows", "snaps"), None), P("rows", None))
    return jax.shard_map(
        per_device,
        mesh=mesh,
        in_specs=placed,
        out_specs=(P("rows", "snaps"), P("rows", "snaps")),
        check_vma=False,
    )
```

profile of v0, /device:TPU:6, one launch (start us, length us, event | category | flops | bytes accessed | tf_op | source)
XLA Modules:
  0.0 176.2 jit_solution(8954403917300474694)
XLA Ops:
  7.2 0.0 copy-start
  7.2 0.0 all-gather.2.cloned.1.call-start
  7.2 0.7 all-gather.2.cloned.1.call-update
  7.9 0.0 reduce-scatter.2.cloned.1.call-start
  8.0 95.2 %all-gather.2.cloned.1.call-done = f32[2048,2048]{1,0:T(8,128)} async-done(((f32[2048,256]{1,0:T(8,128)}), f32[2048,2048]{1,0:T(8,128)}) %all-gather.2.cloned.1.call-update) | async-done | bytes 16777232 | tf_op jit(solution)/shard_map/all_gather | solution.py:26
  103.2 0.0 copy-done
  103.2 19.4 %convolution_bitcast_fusion = f32[2048,256]{0,1:T(8,128)} fusion(f32[2048,2048]{1,0:T(8,128)} %all-gather.2.cloned.1.call-done, f32[2048,256]{1,0:T(8,128)S(1)} %copy-done, f32[2048]{0:T(1024)} %param.5), kind=kOutput, calls=%fused_computation.1 | convolution fusion | flops 12885426176 | bytes 20979712 | tf_op jit(solution)/shard_map/dot_general | solution.py:12
  122.6 0.0 copy-start.1
  122.6 0.0 reduce-scatter.2.cloned.1.call-update
  122.6 1.6 copy-done.1
  124.2 1.8 %copy.8 = f32[256,2048]{0,1:T(8,128)} copy(f32[256,2048]{1,0:T(8,128)S(1)} %copy-done.1) | data formatting | bytes 4194304 | tf_op args[2]
  126.0 0.0 copy-start.2
  126.0 5.2 %all-to-all-start = ((f32[256,8,256]{0,2,1:T(8,128)}), f32[256,8,256]{0,2,1:T(8,128)S(1)}, u32[]{:S(2)}, u32[]{:S(2)}) async-start(f32[256,8,256]{0,2,1:T(8,128)} %bitcast.15), calls=%async_computation.1 | async-start | bytes 4194304 | tf_op jit(solution)/shard_map/all_to_all | solution.py:27
  131.2 0.0 copy-done.2
  131.2 0.1 broadcast_in_dim.15
  131.3 0.1 broadcast_in_dim.16
  131.4 24.1 %all-to-all-done = f32[256,8,256]{0,2,1:T(8,128)S(1)} async-done(((f32[256,8,256]{0,2,1:T(8,128)}), f32[256,8,256]{0,2,1:T(8,128)S(1)}, u32[]{:S(2)}, u32[]{:S(2)}) %all-to-all-start) | async-done | bytes 2097184 | tf_op jit(solution)/shard_map/all_to_all | solution.py:27
  155.4 1.8 %copy.9 = f32[8,256,256]{2,1,0:T(8,128)} copy(f32[8,256,256]{1,2,0:T(8,128)S(1)} %bitcast.14) | data formatting | bytes 4194304 | tf_op jit(solution)/shard_map/all_to_all | solution.py:27
  157.3 2.3 %gather_fusion = f32[64,32,256]{2,1,0:T(8,128)S(1)} fusion(f32[64,32,256]{2,1,0:T(8,128)} %bitcast.16, s32[1024]{0:T(1024)S(1)} %pad_clamp_fusion), kind=kCustom, calls=%fused_computation | custom fusion | bytes 4194560 | tf_op jit(solution)/shard_map/jit(_take)/gather | solution.py:29
  159.5 1.7 bitcast_select_fusion
  161.2 6.1 %reduce-scatter.2.cloned.1.call-done = f32[512,256]{0,1:T(8,128)} async-done(((f32[2048,256]{0,1:T(8,128)}), f32[512,256]{0,1:T(8,128)}) %reduce-scatter.2.cloned.1.call-update) | async-done | bytes 524304 | tf_op jit(solution)/shard_map/reduce_scatter | solution.py:30
  167.3 1.1 broadcast_multiply_fusion
  168.4 1.0 copy.10
  (3 shorter events, 0.0 us)
Async XLA Ops:
  7.2 96.0 %copy-start = (f32[2048,256]{1,0:T(8,128)S(1)}, f32[2048,256]{1,0:T(8,128)}, u32[]{:S(2)}) copy-start(f32[2048,256]{1,0:T(8,128)} %param.4) | copy-start | bytes 6291460
  7.2 96.0 %all-gather.2.cloned.1.call-start = ((), (), s32[]{:S(2)}) async-start(), calls=%async_computation.2 | async-start | bytes 18874368 | tf_op jit(solution)/shard_map/all_gather | solution.py:26
  7.9 159.4 %reduce-scatter.2.cloned.1.call-start = ((), (), s32[]{:S(2)}) async-start(), calls=%async_computation.3 | async-start | bytes 2621440 | tf_op jit(solution)/shard_map/reduce_scatter | solution.py:30
  122.6 1.6 copy-start.1
  126.0 5.2 %copy-start.2 = (s32[1,64]{1,0:T(1,128)S(1)}, s32[1,64]{1,0:T(1,128)}, u32[]{:S(2)}) copy-start(s32[1,64]{1,0:T(1,128)} %param.7) | copy-start | bytes 772
  126.0 29.5 %all-to-all-start = ((f32[256,8,256]{0,2,1:T(8,128)}), f32[256,8,256]{0,2,1:T(8,128)S(1)}, u32[]{:S(2)}, u32[]{:S(2)}) async-start(f32[256,8,256]{0,2,1:T(8,128)} %bitcast.15), calls=%async_computation.1 | async-start | bytes 4194304 | tf_op jit(solution)/shard_map/all_to_all | solution.py:27
Sparse Core Ops, SparseCore 0:
  9.9 93.2 all-gather.1
  122.7 44.5 reduce-scatter.1
where the time goes:
time: 178 us; the launch traced here: 176 us
  waiting for transfers between devices  126 us (71%)
  matrix products  19.4 us (11%)
  between operations  14.1 us (8%)
  local copies, waits for them, and re-layouts  8.62 us (5%)
  starting transfers between devices  5.28 us (3%)
  other arithmetic  2.77 us (2%)
    all_gather x1, waiting for transfers between devices, per_device(): lax.all_gather(snapshots, 'snaps', axis=1, tiled=True)  95.2 us
    all_to_all x1, waiting for transfers between devices, per_device(): lax.all_to_all(next_bricks, 'snaps', split_axis=1, concat_axis=0, tiled=T...  24.1 us
    dot_general x1, matrix products, pair_tile(): lax.dot_general(left, right, (((0,), (0,)), ((), ())), precision=lax.Prec...  19.4 us
    reduce_scatter x1, waiting for transfers between devices, per_device(): summed = lax.psum_scatter(column, 'rows', scatter_dimension=0, tiled=True)  6.11 us
    all_to_all x1, starting transfers between devices, per_device(): lax.all_to_all(next_bricks, 'snaps', split_axis=1, concat_axis=0, tiled=T...  5.2 us
    unnamed x8, local copies, waits for them, and re-layouts  4.37 us
  transfers between devices with their start and end apart: 3, of which 3 were waited for; matrix products, arithmetic and copies ran while one was open for 4% of the time, Pallas kernels for 0%

commit v1 on v0

v1 whole, which is shorter than its diff:
```python
import functools
import math

import jax
import jax.numpy as jnp
from jax import lax
from jax.experimental import pallas as pl
from jax.experimental.pallas import tpu as pltpu
from jax.sharding import PartitionSpec as P

MESH = pl.DeviceIdType.MESH
STEP = 256
PIECES = 2
GROUPS = 8


def split(x):
    hi = x.astype(jnp.bfloat16)
    return hi, (x - hi.astype(jnp.float32)).astype(jnp.bfloat16)


def tdot(a, b):
    return lax.dot_general(a, b, (((0,), (0,)), ((), ())), preferred_element_type=jnp.float32)


def kernel(
    n_r, n_s, scale,
    snap, wts, bricks,
    gram, arrived,
    gbuf, mate, w_hi, w_lo, part, rs_buf, h_send, h_recv,
    ring_send, ring_recv, brick_send, brick_recv, rs_send, rs_recv, d_send, d_recv, own_sem,
):
    n = n_s // 2
    z = lax.axis_index("rows")
    s = lax.axis_index("snaps")
    c = s % 2
    chip = s // 2
    rows, width = snap.shape
    per_brick_dev = bricks.shape[0]

    def ring_of(i):
        u, v = i // 2, i % 2
        return u + v * (n - 1 - 2 * u)

    def chip_at(t):
        v = t // (n // 2)
        return 2 * (t + v * (n - 1 - 2 * t)) + v

    t = ring_of(chip)
    partner = chip * 2 + (1 - c)
    nxt = chip_at((t + 1) % n) * 2 + c
    prv = chip_at((t + n - 1) % n) * 2 + c

    barrier = pltpu.get_barrier_semaphore()
    for k in range(1, n_s):
        pl.semaphore_signal(barrier, inc=1, device_id=(z, (s + k) % n_s), device_id_type=MESH)
    for k in range(1, n_r):
        pl.semaphore_signal(barrier, inc=1, device_id=((z + k) % n_r, s), device_id_type=MESH)
    pl.semaphore_wait(barrier, n_s - 1 + n_r - 1)

    half = rows // 2
    piece = half // PIECES

    def ring_copy(way, hop, q):
        r0 = way * half + q * piece
        there = (n - hop if way == 0 else hop) - 1
        if hop == 1:
            src = snap.at[pl.ds(r0, piece)]
        else:
            here = (n - hop + 1 if way == 0 else hop - 1) - 1
            src = gbuf.at[here, pl.ds(r0, piece)]
        return pltpu.make_async_remote_copy(
            src_ref=src,
            dst_ref=gbuf.at[there, pl.ds(r0, piece)],
            send_sem=ring_send.at[way, hop - 1, q],
            recv_sem=ring_recv.at[way, hop - 1, q],
            device_id=(z, nxt if way == 0 else prv),
            device_id_type=MESH,
        )

    def brick_copy(k):
        to = (s + k) % n_s
        return pltpu.make_async_remote_copy(
            src_ref=bricks.at[:, pl.ds(pl.multiple_of(to * width, width), width)],
            dst_ref=arrived.at[pl.ds(pl.multiple_of(s * per_brick_dev, per_brick_dev), per_brick_dev)],
            send_sem=brick_send.at[k - 1],
            recv_sem=brick_recv.at[k - 1],
            device_id=(z, to),
            device_id_type=MESH,
        )

    def rs_copy(slot, k, home):
        return pltpu.make_async_remote_copy(
            src_ref=part.at[slot],
            dst_ref=rs_buf.at[k - 1],
            send_sem=rs_send.at[k - 1],
            recv_sem=rs_recv.at[k - 1],
            device_id=(home, s),
            device_id_type=MESH,
        )

    def d2d(i, src, dst):
        return pltpu.make_async_remote_copy(
            src_ref=src, dst_ref=dst, send_sem=d_send.at[i], recv_sem=d_recv.at[i],
            device_id=(z, partner), device_id_type=MESH,
        )

    for q in range(PIECES):
        for way in range(2):
            ring_copy(way, 1, q).start()
    own_bricks = pltpu.make_async_copy(
        bricks.at[:, pl.ds(pl.multiple_of(s * width, width), width)],
        arrived.at[pl.ds(pl.multiple_of(s * per_brick_dev, per_brick_dev), per_brick_dev)],
        own_sem.at[0],
    )
    own_bricks.start()
    to_mate = d2d(0, snap, mate)
    to_mate.start()

    def weigh(src, col):
        def body(i, carry):
            r0 = pl.multiple_of(i * 128, 128)
            w = jnp.broadcast_to(wts[pl.ds(i, 1), :], (128, 128)).T
            for l in range(width // 128):
                hi, lo = split(src[pl.ds(r0, 128), l * 128:(l + 1) * 128] * w)
                w_hi[pl.ds(r0, 128), col + l * 128:col + (l + 1) * 128] = hi
                w_lo[pl.ds(r0, 128), col + l * 128:col + (l + 1) * 128] = lo
            return carry
        lax.fori_loop(0, rows // 128, body, 0)

    def gather_product(slot, load, r0, count):
        def body(i, carry):
            r = pl.multiple_of(r0 + i * STEP, STEP)
            hi, lo = split(load(r))
            bh = w_hi[pl.ds(r, STEP), :]
            bl = w_lo[pl.ds(r, STEP), :]
            part[slot] += tdot(hi, bh) + (tdot(hi, bl) + tdot(lo, bh))
            return carry
        lax.fori_loop(0, count // STEP, body, 0)

    def send_home(slot):
        home = chip_at((t + slot) % n)
        k = (home + n_r - z) % n_r

        @pl.when(k > 0)
        def _():
            rs_copy(slot, k, home).start()

    weigh(snap, 0)
    part[...] = jnp.zeros_like(part)
    to_mate.wait()
    weigh(mate, width)
    gather_product(0, lambda r: snap[pl.ds(r, STEP), :], 0, rows)
    send_home(0)

    done = [0] * n
    for hop in range(1, n):
        for q in range(PIECES):
            for way in range(2):
                ring_copy(way, hop, q).wait_recv()
                if hop < n - 1:
                    ring_copy(way, hop + 1, q).start()
            if q == PIECES - 1 and hop == n - 2:
                for k in range(1, n_s):
                    brick_copy(k).start()
            for way in range(2):
                slot = n - hop if way == 0 else hop
                gather_product(
                    slot,
                    lambda r, slot=slot: gbuf[slot - 1, pl.ds(r, STEP), :],
                    way * half + q * piece,
                    piece,
                )
        for way in range(2):
            slot = n - hop if way == 0 else hop
            done[slot] += 1
            if done[slot] == 2:
                send_home(slot)

    for k in range(1, n_r):
        rs_copy(0, k, (z + k) % n_r).wait_recv()
    own = (ring_of(z) + n - t) % n
    total = part[own]
    for k in range(1, n_r):
        total += rs_buf[k - 1]
    total = total / scale
    h_send[...] = total[:, width:]
    to_other = d2d(1, h_send, h_recv)
    to_other.start()
    gram[pl.ds(pl.multiple_of(c * width, width), width), :] = total[:, :width]

    for k in range(1, n_s):
        brick_copy(k).wait_recv()
    own_bricks.wait()
    to_other.wait()
    gram[pl.ds(pl.multiple_of((1 - c) * width, width), width), :] = h_recv[...]
    for hop in range(1, n):
        for q in range(PIECES):
            for way in range(2):
                ring_copy(way, hop, q).wait_send()
    for k in range(1, n_s):
        brick_copy(k).wait_send()
    for k in range(1, n_r):
        rs_copy(0, k, (z + k) % n_r).wait_send()


def place_bricks(n_bricks, order, src, dst, buf, in_sem, out_sem):
    tall = src.shape[0] // n_bricks
    group = n_bricks // GROUPS

    def fetch(i):
        return pltpu.make_async_copy(
            src.at[pl.ds(pl.multiple_of(order[0, i] * tall, tall), tall)],
            buf.at[pl.ds(pl.multiple_of(i * tall, tall), tall)],
            in_sem.at[i],
        )

    def put(g):
        block = pl.ds(g * group * tall, group * tall)
        return pltpu.make_async_copy(buf.at[block], dst.at[block], out_sem.at[g])

    def start(i, carry):
        fetch(i).start()
        return carry

    def wait(i, carry):
        fetch(i).wait()
        return carry

    lax.fori_loop(0, n_bricks, start, 0)
    for g in range(GROUPS):
        lax.fori_loop(g * group, (g + 1) * group, wait, 0)
        put(g).start()
    for g in range(GROUPS):
        put(g).wait()


def per_device(n_r, n_s, snapshots, weights, next_bricks, brick_source):
    rows, width = snapshots.shape
    n = n_s // 2
    assert n == n_r and n % 2 == 0
    f32, bf16 = jnp.float32, jnp.bfloat16
    vmem = pl.BlockSpec(memory_space=pltpu.VMEM)
    dma = pltpu.SemaphoreType.DMA
    gram, arrived = pl.pallas_call(
        functools.partial(kernel, n_r, n_s, math.sqrt(rows * n_r)),
        out_shape=(
            jax.ShapeDtypeStruct((n_s * width // n_r, width), f32),
            jax.ShapeDtypeStruct((rows, width), f32),
        ),
        in_specs=[vmem, vmem, vmem],
        out_specs=(vmem, pl.BlockSpec(memory_space=pl.ANY)),
        scratch_shapes=[
            pltpu.VMEM((n - 1, rows, width), f32),
            pltpu.VMEM((rows, width), f32),
            pltpu.VMEM((rows, 2 * width), bf16),
            pltpu.VMEM((rows, 2 * width), bf16),
            pltpu.VMEM((n, width, 2 * width), f32),
            pltpu.VMEM((n_r - 1, width, 2 * width), f32),
            pltpu.VMEM((width, width), f32),
            pltpu.VMEM((width, width), f32),
            dma((2, n - 1, PIECES)),
            dma((2, n - 1, PIECES)),
            dma((n_s - 1,)),
            dma((n_s - 1,)),
            dma((n_r - 1,)),
            dma((n_r - 1,)),
            dma((2,)),
            dma((2,)),
            dma((1,)),
        ],
        compiler_params=pltpu.CompilerParams(
            collective_id=0, has_side_effects=True, vmem_limit_bytes=62 * 1024 * 1024
        ),
    )(snapshots, weights.reshape(-1, 128), next_bricks)
    n_bricks = brick_source.shape[1]
    tiles = pl.pallas_call(
        functools.partial(place_bricks, n_bricks),
        out_shape=jax.ShapeDtypeStruct((rows, width), f32),
        in_specs=[pl.BlockSpec(memory_space=pltpu.SMEM), pl.BlockSpec(memory_space=pl.ANY)],
        out_specs=pl.BlockSpec(memory_space=pl.ANY),
        scratch_shapes=[pltpu.VMEM((rows, width), f32), dma((n_bricks,)), dma((GROUPS,))],
    )(brick_source, arrived)
    return gram, tiles


def solution(mesh):
    placed = (P("rows", "snaps"), P("rows"), P(("rows", "snaps"), None), P("rows", None))
    return jax.shard_map(
        functools.partial(per_device, mesh.shape["rows"], mesh.shape["snaps"]),
        mesh=mesh,
        in_specs=placed,
        out_specs=(P("rows", "snaps"), P("rows", "snaps")),
        check_vma=False,
    )
```

time: 178 us -> 119 us (0.67)
  the two profiles are of different devices: /device:TPU:6 before, /device:TPU:3 now
where the time goes in v1:
time: 119 us
  Pallas kernels  118 us (99%)
    pallas_call x1, Pallas kernels, per_device(): pl.pallas_call(functools.partial(kernel, n_r, n_s, math.sqrt(rows * n_r))...  114 us
    pallas_call x1, Pallas kernels, per_device(): pl.pallas_call(functools.partial(place_bricks, n_bricks), out_shape=jax.S...  3.69 us

profile of v1, /device:TPU:3, one launch (start us, length us, event | category | flops | bytes accessed | tf_op | source)
XLA Modules:
  0.0 119.2 jit_solution(18277578565572598006)
XLA Ops:
  0.6 114.1 %shard_map.59 = (f32[512,256]{1,0:T(8,128)}, f32[2048,256]{1,0:T(8,128)}) custom-call(f32[2048,256]{1,0:T(8,128)} %snap.1, f32[16,128]{1,0:T(8,128)} %bitcast.1, f32[256,2048]{1,0:T(8,128)} %bricks.1), custom_call_target="tpu_custom_call" | custom-call | tf_op jit(solution)/shard_map/pallas_call | solution.py:245
  114.7 0.0 copy-start
  114.7 3.7 %shard_map.60 = f32[2048,256]{1,0:T(8,128)} custom-call(s32[1,64]{1,0:T(1,128)} %order.1, f32[2048,256]{1,0:T(8,128)} %get-tuple-element.5.src), custom_call_target="tpu_custom_call" | custom-call | tf_op jit(solution)/shard_map/pallas_call | solution.py:277
  118.4 0.0 copy-done
  118.4 0.8 copy.7
Async XLA Ops:
  114.7 3.7 %copy-start = (f32[512,256]{1,0:T(8,128)S(1)}, f32[512,256]{1,0:T(8,128)}, u32[]{:S(2)}) copy-start(f32[512,256]{1,0:T(8,128)} %get-tuple-element.8) | copy-start | bytes 1572868

commit v2 on v1

--- a/solution.py
+++ b/solution.py
@@ -204,6 +204,287 @@
         rs_copy(0, k, (z + k) % n_r).wait_send()
 
 
+def folded_kernel(
+    n_r, n_s, scale,
+    snap, wts, bricks,
+    gram, arrived,
+    gbuf, mate, w_hi, w_lo, part, rs_buf, quad, xbuf, fin, fbuf,
+    ring_send, ring_recv, brick_send, brick_recv, rs_send, rs_recv,
+    x_send, x_recv, f_send, f_recv, d_send, d_recv, own_sem,
+):
+    n = n_s // 2
+    z = lax.axis_index("rows")
+    s = lax.axis_index("snaps")
+    c = s % 2
+    chip = s // 2
+    rows, width = snap.shape
+    per_brick_dev = bricks.shape[0]
+
+    def ring_of(i):
+        u, v = i // 2, i % 2
+        return u + v * (n - 1 - 2 * u)
+
+    def chip_at(t):
+        v = t // (n // 2)
+        return 2 * (t + v * (n - 1 - 2 * t)) + v
+
+    t = ring_of(chip)
+    partner = chip * 2 + (1 - c)
+    nxt = chip_at((t + 1) % n) * 2 + c
+    prv = chip_at((t + n - 1) % n) * 2 + c
+
+    barrier = pltpu.get_barrier_semaphore()
+    for k in range(1, n_s):
+        pl.semaphore_signal(barrier, inc=1, device_id=(z, (s + k) % n_s), device_id_type=MESH)
+    for k in range(1, n_r):
+        for who in (s, partner):
+            pl.semaphore_signal(barrier, inc=1, device_id=((z + k) % n_r, who), device_id_type=MESH)
+    pl.semaphore_wait(barrier, n_s - 1 + 2 * (n_r - 1))
+
+    half = rows // 2
+    piece = half // 2
+
+    def start_of(way, owner, other):
+        q = owner // 2
+        q = q + other * (1 - 2 * q)
+        return pl.multiple_of(way * half + q * piece, piece)
+
+    def ring_copy(way, stage):
+        if stage < 2:
+            r0 = start_of(way, t, stage)
+            src = snap.at[pl.ds(r0, piece)]
+            there = n - 1 if way == 0 else 1
+        else:
+            owner = (t + n - 1) % n if way == 0 else (t + 1) % n
+            r0 = start_of(way, owner, 0)
+            src = gbuf.at[n - 2 if way == 0 else 0, pl.ds(r0, piece)]
+            there = 2
+        return pltpu.make_async_remote_copy(
+            src_ref=src,
+            dst_ref=gbuf.at[there - 1, pl.ds(r0, piece)],
+            send_sem=ring_send.at[way, stage],
+            recv_sem=ring_recv.at[way, stage],
+            device_id=(z, nxt if way == 0 else prv),
+            device_id_type=MESH,
+        )
+
+    def brick_copy(k):
+        to = (s + k) % n_s
+        return pltpu.make_async_remote_copy(
+            src_ref=bricks.at[:, pl.ds(pl.multiple_of(to * width, width), width)],
+            dst_ref=arrived.at[pl.ds(pl.multiple_of(s * per_brick_dev, per_brick_dev), per_brick_dev)],
+            send_sem=brick_send.at[k - 1],
+            recv_sem=brick_recv.at[k - 1],
+            device_id=(z, to),
+            device_id_type=MESH,
+        )
+
+    def level_of(other, row_core, col_core):
+        low = jnp.where(chip <= other, 1, 0)
+        return low * (2 * row_core + col_core) + (1 - low) * (2 * col_core + row_core)
+
+    def chunk(d):
+        return chip_at((t + d) % n)
+
+    def col_core_here(d):
+        low = jnp.where(chip <= chunk(d), 1, 0)
+        return low * (z % 2) + (1 - low) * (z // 2)
+
+    def holds(d):
+        low = jnp.where(chip <= chunk(d), 1, 0)
+        return low * (z // 2) + (1 - low) * (z % 2) == c
+
+    def rs_copy(d, side, k, home):
+        return pltpu.make_async_remote_copy(
+            src_ref=part.at[d, :, pl.ds(side * width, width)],
+            dst_ref=rs_buf.at[d, k - 1],
+            send_sem=rs_send.at[d, side],
+            recv_sem=rs_recv.at[d, k - 1],
+            device_id=(home, s),
+            device_id_type=MESH,
+        )
+
+    def x_copy(d):
+        return pltpu.make_async_remote_copy(
+            src_ref=quad.at[d],
+            dst_ref=xbuf.at[n - d - 1],
+            send_sem=x_send.at[d - 1],
+            recv_sem=x_recv.at[n - d - 1],
+            device_id=(z, chunk(d) * 2 + col_core_here(d)),
+            device_id_type=MESH,
+        )
+
+    def x_arrival(d):
+        return pltpu.make_async_remote_copy(
+            src_ref=quad.at[d],
+            dst_ref=xbuf.at[d - 1],
+            send_sem=x_send.at[d - 1],
+            recv_sem=x_recv.at[d - 1],
+            device_id=(z, chunk(d) * 2 + col_core_here(d)),
+            device_id_type=MESH,
+        )
+
+    def f_copy(d):
+        return pltpu.make_async_remote_copy(
+            src_ref=fin.at[d],
+            dst_ref=fbuf.at[c],
+            send_sem=f_send.at[d],
+            recv_sem=f_recv.at[c],
+            device_id=(chunk(d), chip * 2 + col_core_here(d)),
+            device_id_type=MESH,
+        )
+
+    def f_arrival(a):
+        return pltpu.make_async_remote_copy(
+            src_ref=fin.at[0],
+            dst_ref=fbuf.at[a],
+            send_sem=f_send.at[0],
+            recv_sem=f_recv.at[a],
+            device_id=((z + 1) % n_r, s),
+            device_id_type=MESH,
+        )
+
+    for stage in range(2):
+        for way in range(2):
+            ring_copy(way, stage).start()
+    own_bricks = pltpu.make_async_copy(
+        bricks.at[:, pl.ds(pl.multiple_of(s * width, width), width)],
+        arrived.at[pl.ds(pl.multiple_of(s * per_brick_dev, per_brick_dev), per_brick_dev)],
+        own_sem.at[0],
+    )
+    own_bricks.start()
+    to_mate = pltpu.make_async_remote_copy(
+        src_ref=snap, dst_ref=mate, send_sem=d_send.at[0], recv_sem=d_recv.at[0],
+        device_id=(z, partner), device_id_type=MESH,
+    )
+    to_mate.start()
+
+    def weigh(src, col):
+        def body(i, carry):
+            r0 = pl.multiple_of(i * 128, 128)
+            w = jnp.broadcast_to(wts[pl.ds(i, 1), :], (128, 128)).T
+            for l in range(width // 128):
+                hi, lo = split(src[pl.ds(r0, 128), l * 128:(l + 1) * 128] * w)
+                w_hi[pl.ds(r0, 128), col + l * 128:col + (l + 1) * 128] = hi
+                w_lo[pl.ds(r0, 128), col + l * 128:col + (l + 1) * 128] = lo
+            return carry
+        lax.fori_loop(0, rows // 128, body, 0)
+
+    def gather_product(slot, load, r0, count):
+        def body(i, carry):
+            r = pl.multiple_of(r0 + i * STEP, STEP)
+            hi, lo = split(load(r))
+            bh = w_hi[pl.ds(r, STEP), :]
+            bl = w_lo[pl.ds(r, STEP), :]
+            part[slot] += tdot(hi, bh) + (tdot(hi, bl) + tdot(lo, bh))
+            return carry
+        lax.fori_loop(0, count // STEP, body, 0)
+
+    def take(slot, r0):
+        gather_product(slot, lambda r: gbuf[slot - 1, pl.ds(r, STEP), :], r0, piece)
+
+    def sides(d, act):
+        for side in range(2):
+            home = level_of(chunk(d), c, (c + side) % 2)
+            k = (home + n_r - z) % n_r
+
+            @pl.when(k > 0)
+            def _():
+                act(rs_copy(d, side, k, home))
+
+    weigh(snap, 0)
+    part[...] = jnp.zeros_like(part)
+    to_mate.wait()
+    weigh(mate, width)
+    gather_product(0, lambda r: snap[pl.ds(r, STEP), :], 0, rows)
+    sides(0, lambda copy: copy.start())
+
+    near = ((0, n - 1, (t + n - 1) % n), (1, 1, (t + 1) % n))
+    for way, slot, owner in near:
+        ring_copy(way, 0).wait_recv()
+        ring_copy(way, 2).start()
+    for way, slot, owner in near:
+        take(slot, start_of(way, owner, 0))
+    for way, slot, owner in near:
+        ring_copy(way, 1).wait_recv()
+    for k in range(1, n_s):
+        brick_copy(k).start()
+    for way, slot, owner in near:
+        take(slot, start_of(way, owner, 1))
+        sides(slot, lambda copy: copy.start())
+    for way in range(2):
+        ring_copy(way, 2).wait_recv()
+        take(2, start_of(way, (t + 2) % n, 0))
+    sides(2, lambda copy: copy.start())
+
+    def finish(d):
+        col_core = col_core_here(d)
+        home = chunk(d)
+        here = jnp.where(home == z, 1, 0) * jnp.where(col_core == c, 1, 0)
+
+        @pl.when(here == 0)
+        def _():
+            f_copy(d).start()
+
+        @pl.when(here == 1)
+        def _():
+            fbuf[c] = fin[d]
+
+    order = (0, 1, 3, 2)
+    for d in order:
+        @pl.when(holds(d))
+        def _():
+            for k in range(1, n_r):
+                rs_copy(d, 0, k, (z + k) % n_r).wait_recv()
+            side = (col_core_here(d) + c) % 2
+            total = part[d, :, pl.ds(pl.multiple_of(side * width, width), width)]
+            for k in range(1, n_r):
+                total += rs_buf[d, k - 1]
+            if d == 0:
+                fin[0] = total / scale
+                finish(0)
+            else:
+                quad[d] = total
+                x_copy(d).start()
+    for d in order[1:]:
+        @pl.when(holds(d))
+        def _():
+            x_arrival(d).wait_recv()
+            fin[d] = (quad[d] + xbuf[d - 1].T) / scale
+            finish(d)
+
+    for k in range(1, n_s):
+        brick_copy(k).wait_recv()
+    own_bricks.wait()
+    for a in range(2):
+        level = level_of(z, a, c)
+        same = jnp.where(level == z, 1, 0) * jnp.where(c == a, 1, 0)
+
+        @pl.when(same == 0)
+        def _():
+            f_arrival(a).wait_recv()
+
+        gram[a * width:(a + 1) * width, :] = fbuf[a]
+
+    for way in range(2):
+        for stage in range(3):
+            ring_copy(way, stage).wait_send()
+    for k in range(1, n_s):
+        brick_copy(k).wait_send()
+    for d in range(n):
+        sides(d, lambda copy: copy.wait_send())
+
+        @pl.when(holds(d))
+        def _():
+            if d > 0:
+                x_copy(d).wait_send()
+            here = jnp.where(chunk(d) == z, 1, 0) * jnp.where(col_core_here(d) == c, 1, 0)
+
+            @pl.when(here == 0)
+            def _():
+                f_copy(d).wait_send()
+
+
 def place_bricks(n_bricks, order, src, dst, buf, in_sem, out_sem):
     tall = src.shape[0] // n_bricks
     group = n_bricks // GROUPS
@@ -242,21 +523,39 @@
     f32, bf16 = jnp.float32, jnp.bfloat16
     vmem = pl.BlockSpec(memory_space=pltpu.VMEM)
     dma = pltpu.SemaphoreType.DMA
-    gram, arrived = pl.pallas_call(
-        functools.partial(kernel, n_r, n_s, math.sqrt(rows * n_r)),
-        out_shape=(
-            jax.ShapeDtypeStruct((n_s * width // n_r, width), f32),
-            jax.ShapeDtypeStruct((rows, width), f32),
-        ),
-        in_specs=[vmem, vmem, vmem],
-        out_specs=(vmem, pl.BlockSpec(memory_space=pl.ANY)),
-        scratch_shapes=[
-            pltpu.VMEM((n - 1, rows, width), f32),
-            pltpu.VMEM((rows, width), f32),
-            pltpu.VMEM((rows, 2 * width), bf16),
-            pltpu.VMEM((rows, 2 * width), bf16),
-            pltpu.VMEM((n, width, 2 * width), f32),
-            pltpu.VMEM((n_r - 1, width, 2 * width), f32),
+    wide = 2 * width
+    scratch = [
+        pltpu.VMEM((n - 1, rows, width), f32),
+        pltpu.VMEM((rows, width), f32),
+        pltpu.VMEM((rows, wide), bf16),
+        pltpu.VMEM((rows, wide), bf16),
+        pltpu.VMEM((n, width, wide), f32),
+    ]
+    folded = n == 4
+    if folded:
+        scratch += [
+            pltpu.VMEM((n, n_r - 1, width, width), f32),
+            pltpu.VMEM((n, width, width), f32),
+            pltpu.VMEM((n - 1, width, width), f32),
+            pltpu.VMEM((n, width, width), f32),
+            pltpu.VMEM((2, width, width), f32),
+            dma((2, 3)),
+            dma((2, 3)),
+            dma((n_s - 1,)),
+            dma((n_s - 1,)),
+            dma((n, 2)),
+            dma((n, n_r - 1)),
+            dma((n - 1,)),
+            dma((n - 1,)),
+            dma((n,)),
+            dma((2,)),
+            dma((1,)),
+            dma((1,)),
+            dma((1,)),
+        ]
+    else:
+        scratch += [
+            pltpu.VMEM((n_r - 1, width, wide), f32),
             pltpu.VMEM((width, width), f32),
             pltpu.VMEM((width, width), f32),
             dma((2, n - 1, PIECES)),
@@ -268,7 +567,16 @@
             dma((2,)),
             dma((2,)),
             dma((1,)),
-        ],
+        ]
+    gram, arrived = pl.pallas_call(
+        functools.partial(folded_kernel if folded else kernel, n_r, n_s, math.sqrt(rows * n_r)),
+        out_shape=(
+            jax.ShapeDtypeStruct((n_s * width // n_r, width), f32),
+            jax.ShapeDtypeStruct((rows, width), f32),
+        ),
+        in_specs=[vmem, vmem, vmem],
+        out_specs=(vmem, pl.BlockSpec(memory_space=pl.ANY)),
+        scratch_shapes=scratch,
         compiler_params=pltpu.CompilerParams(
             collective_id=0, has_side_effects=True, vmem_limit_bytes=62 * 1024 * 1024
         ),

time: 119 us -> 95.6 us (0.80)
  the two profiles are of different devices: /device:TPU:3 before, /device:TPU:6 now
where the time goes in v2:
time: 95.6 us; the launch traced here: 94.9 us
  Pallas kernels  93.5 us (98%)
    pallas_call x1, Pallas kernels, per_device(): pl.pallas_call(functools.partial(folded_kernel if folded else kernel, n_r...  89.8 us
    pallas_call x1, Pallas kernels, per_device(): pl.pallas_call(functools.partial(place_bricks, n_bricks), out_shape=jax.S...  3.69 us

profile of v2, /device:TPU:6, one launch (start us, length us, event | category | flops | bytes accessed | tf_op | source)
XLA Modules:
  0.0 94.9 jit_solution(14154143593318978272)
XLA Ops:
  0.6 89.8 %shard_map.59 = (f32[512,256]{1,0:T(8,128)}, f32[2048,256]{1,0:T(8,128)}) custom-call(f32[2048,256]{1,0:T(8,128)} %snap.1, f32[16,128]{1,0:T(8,128)} %bitcast.1, f32[256,2048]{1,0:T(8,128)} %bricks.1), custom_call_target="tpu_custom_call" | custom-call | tf_op jit(solution)/shard_map/pallas_call | solution.py:571
  90.4 0.0 copy-start
  90.4 3.7 %shard_map.60 = f32[2048,256]{1,0:T(8,128)} custom-call(s32[1,64]{1,0:T(1,128)} %order.1, f32[2048,256]{1,0:T(8,128)} %get-tuple-element.5.src), custom_call_target="tpu_custom_call" | custom-call | tf_op jit(solution)/shard_map/pallas_call | solution.py:585
  94.1 0.0 copy-done
  94.1 0.8 copy.7
Async XLA Ops:
  90.4 3.7 %copy-start = (f32[512,256]{1,0:T(8,128)S(1)}, f32[512,256]{1,0:T(8,128)}, u32[]{:S(2)}) copy-start(f32[512,256]{1,0:T(8,128)} %get-tuple-element.8) | copy-start | bytes 1572868

commit v3 on v2

--- a/solution.py
+++ b/solution.py
@@ -206,18 +206,18 @@
 
 def folded_kernel(
     n_r, n_s, scale,
-    snap, wts, bricks,
+    snap_in, wts, bricks,
     gram, arrived,
-    gbuf, mate, w_hi, w_lo, part, rs_buf, quad, xbuf, fin, fbuf,
+    snap, bounce, gbuf, mate, w_hi, w_lo, part, rs_buf, quad, xbuf, fin, fbuf,
     ring_send, ring_recv, brick_send, brick_recv, rs_send, rs_recv,
-    x_send, x_recv, f_send, f_recv, d_send, d_recv, own_sem,
+    x_send, x_recv, f_send, f_recv, d_send, d_recv, own_sem, in_sem,
 ):
     n = n_s // 2
     z = lax.axis_index("rows")
     s = lax.axis_index("snaps")
     c = s % 2
     chip = s // 2
-    rows, width = snap.shape
+    rows, width = snap_in.shape
     per_brick_dev = bricks.shape[0]
 
     def ring_of(i):
@@ -233,12 +233,19 @@
     nxt = chip_at((t + 1) % n) * 2 + c
     prv = chip_at((t + n - 1) % n) * 2 + c
 
+    load_snap = pltpu.make_async_copy(snap_in, snap, in_sem.at[0])
+    load_snap.start()
+    own_bricks_in = pltpu.make_async_copy(
+        bricks.at[:, pl.ds(pl.multiple_of(s * width, width), width)], bounce, in_sem.at[1]
+    )
+    own_bricks_in.start()
     barrier = pltpu.get_barrier_semaphore()
     for k in range(1, n_s):
         pl.semaphore_signal(barrier, inc=1, device_id=(z, (s + k) % n_s), device_id_type=MESH)
     for k in range(1, n_r):
         for who in (s, partner):
             pl.semaphore_signal(barrier, inc=1, device_id=((z + k) % n_r, who), device_id_type=MESH)
+    load_snap.wait()
     pl.semaphore_wait(barrier, n_s - 1 + 2 * (n_r - 1))
 
     half = rows // 2
@@ -249,22 +256,28 @@
         q = q + other * (1 - 2 * q)
         return pl.multiple_of(way * half + q * piece, piece)
 
+    def slot_of(way):
+        return n - 1 - way * (n - 2)
+
+    def owner_of(way):
+        return (t + n - 1 + 2 * way) % n
+
     def ring_copy(way, stage):
         if stage < 2:
             r0 = start_of(way, t, stage)
             src = snap.at[pl.ds(r0, piece)]
-            there = n - 1 if way == 0 else 1
+            there = n - 1 - way * (n - 2)
         else:
-            owner = (t + n - 1) % n if way == 0 else (t + 1) % n
+            owner = owner_of(way)
             r0 = start_of(way, owner, 0)
-            src = gbuf.at[n - 2 if way == 0 else 0, pl.ds(r0, piece)]
+            src = gbuf.at[slot_of(way) - 1, pl.ds(r0, piece)]
             there = 2
         return pltpu.make_async_remote_copy(
             src_ref=src,
             dst_ref=gbuf.at[there - 1, pl.ds(r0, piece)],
             send_sem=ring_send.at[way, stage],
             recv_sem=ring_recv.at[way, stage],
-            device_id=(z, nxt if way == 0 else prv),
+            device_id=(z, nxt + way * (prv - nxt)),
             device_id_type=MESH,
         )
 
@@ -344,11 +357,12 @@
             device_id_type=MESH,
         )
 
+    first, second = c, 1 - c
     for stage in range(2):
-        for way in range(2):
-            ring_copy(way, stage).start()
+        ring_copy(first, stage).start()
+    own_bricks_in.wait()
     own_bricks = pltpu.make_async_copy(
-        bricks.at[:, pl.ds(pl.multiple_of(s * width, width), width)],
+        bounce,
         arrived.at[pl.ds(pl.multiple_of(s * per_brick_dev, per_brick_dev), per_brick_dev)],
         own_sem.at[0],
     )
@@ -399,24 +413,6 @@
     gather_product(0, lambda r: snap[pl.ds(r, STEP), :], 0, rows)
     sides(0, lambda copy: copy.start())
 
-    near = ((0, n - 1, (t + n - 1) % n), (1, 1, (t + 1) % n))
-    for way, slot, owner in near:
-        ring_copy(way, 0).wait_recv()
-        ring_copy(way, 2).start()
-    for way, slot, owner in near:
-        take(slot, start_of(way, owner, 0))
-    for way, slot, owner in near:
-        ring_copy(way, 1).wait_recv()
-    for k in range(1, n_s):
-        brick_copy(k).start()
-    for way, slot, owner in near:
-        take(slot, start_of(way, owner, 1))
-        sides(slot, lambda copy: copy.start())
-    for way in range(2):
-        ring_copy(way, 2).wait_recv()
-        take(2, start_of(way, (t + 2) % n, 0))
-    sides(2, lambda copy: copy.start())
-
     def finish(d):
         col_core = col_core_here(d)
         home = chunk(d)
@@ -430,8 +426,7 @@
         def _():
             fbuf[c] = fin[d]
 
-    order = (0, 1, 3, 2)
-    for d in order:
+    def reduce_quadrant(d):
         @pl.when(holds(d))
         def _():
             for k in range(1, n_r):
@@ -446,7 +441,40 @@
             else:
                 quad[d] = total
                 x_copy(d).start()
-    for d in order[1:]:
+    def near(way):
+        for stage in range(2):
+            ring_copy(way, stage).wait_recv()
+        slot = slot_of(way)
+        for stage in range(2):
+            take(slot, start_of(way, owner_of(way), stage))
+        sides(slot, lambda copy: copy.start())
+
+    for stage in range(2):
+        ring_copy(first, stage).wait_send()
+        ring_copy(second, stage).start()
+    near(first)
+    reduce_quadrant(0)
+    for stage in range(2):
+        ring_copy(second, stage).wait_send()
+        if stage == 0:
+            ring_copy(first, 2).start()
+    ring_copy(second, 0).wait_recv()
+    ring_copy(second, 2).start()
+    for k in range(1, n_s):
+        brick_copy(k).start()
+    ring_copy(second, 1).wait_recv()
+    for stage in range(2):
+        take(slot_of(second), start_of(second, owner_of(second), stage))
+    sides(slot_of(second), lambda copy: copy.start())
+    for way in range(2):
+        ring_copy(way, 2).wait_recv()
+        take(2, start_of(way, (t + 2) % n, 0))
+    sides(2, lambda copy: copy.start())
+
+    order = (1, 3, 2)
+    for d in order:
+        reduce_quadrant(d)
+    for d in order:
         @pl.when(holds(d))
         def _():
             x_arrival(d).wait_recv()
@@ -467,8 +495,7 @@
         gram[a * width:(a + 1) * width, :] = fbuf[a]
 
     for way in range(2):
-        for stage in range(3):
-            ring_copy(way, stage).wait_send()
+        ring_copy(way, 2).wait_send()
     for k in range(1, n_s):
         brick_copy(k).wait_send()
     for d in range(n):
@@ -485,7 +512,9 @@
                 f_copy(d).wait_send()
 
 
-def place_bricks(n_bricks, order, src, dst, buf, in_sem, out_sem):
+def place_bricks(n_bricks, order, src, gram, dst, gram_out, buf, gram_buf, in_sem, out_sem, g_sem):
+    gram_in = pltpu.make_async_copy(gram, gram_buf, g_sem.at[0])
+    gram_in.start()
     tall = src.shape[0] // n_bricks
     group = n_bricks // GROUPS
 
@@ -512,8 +541,12 @@
     for g in range(GROUPS):
         lax.fori_loop(g * group, (g + 1) * group, wait, 0)
         put(g).start()
+    gram_in.wait()
+    gram_put = pltpu.make_async_copy(gram_buf, gram_out, g_sem.at[1])
+    gram_put.start()
     for g in range(GROUPS):
         put(g).wait()
+    gram_put.wait()
 
 
 def per_device(n_r, n_s, snapshots, weights, next_bricks, brick_source):
@@ -524,6 +557,7 @@
     vmem = pl.BlockSpec(memory_space=pltpu.VMEM)
     dma = pltpu.SemaphoreType.DMA
     wide = 2 * width
+    hbm = pl.BlockSpec(memory_space=pl.ANY)
     scratch = [
         pltpu.VMEM((n - 1, rows, width), f32),
         pltpu.VMEM((rows, width), f32),
@@ -533,7 +567,7 @@
     ]
     folded = n == 4
     if folded:
-        scratch += [
+        scratch = [pltpu.VMEM((rows, width), f32), pltpu.VMEM((rows // n_s, width), f32)] + scratch + [
             pltpu.VMEM((n, n_r - 1, width, width), f32),
             pltpu.VMEM((n, width, width), f32),
             pltpu.VMEM((n - 1, width, width), f32),
@@ -552,6 +586,7 @@
             dma((1,)),
             dma((1,)),
             dma((1,)),
+            dma((2,)),
         ]
     else:
         scratch += [
@@ -574,21 +609,30 @@
             jax.ShapeDtypeStruct((n_s * width // n_r, width), f32),
             jax.ShapeDtypeStruct((rows, width), f32),
         ),
-        in_specs=[vmem, vmem, vmem],
-        out_specs=(vmem, pl.BlockSpec(memory_space=pl.ANY)),
+        in_specs=[hbm, vmem, hbm] if folded else [vmem, vmem, vmem],
+        out_specs=(vmem, hbm),
         scratch_shapes=scratch,
         compiler_params=pltpu.CompilerParams(
             collective_id=0, has_side_effects=True, vmem_limit_bytes=62 * 1024 * 1024
         ),
     )(snapshots, weights.reshape(-1, 128), next_bricks)
     n_bricks = brick_source.shape[1]
-    tiles = pl.pallas_call(
+    tiles, gram = pl.pallas_call(
         functools.partial(place_bricks, n_bricks),
-        out_shape=jax.ShapeDtypeStruct((rows, width), f32),
-        in_specs=[pl.BlockSpec(memory_space=pltpu.SMEM), pl.BlockSpec(memory_space=pl.ANY)],
-        out_specs=pl.BlockSpec(memory_space=pl.ANY),
-        scratch_shapes=[pltpu.VMEM((rows, width), f32), dma((n_bricks,)), dma((GROUPS,))],
-    )(brick_source, arrived)
+        out_shape=(
+            jax.ShapeDtypeStruct((rows, width), f32),
+            jax.ShapeDtypeStruct(gram.shape, f32),
+        ),
+        in_specs=[pl.BlockSpec(memory_space=pltpu.SMEM), hbm, hbm],
+        out_specs=(hbm, hbm),
+        scratch_shapes=[
+            pltpu.VMEM((rows, width), f32),
+            pltpu.VMEM(gram.shape, f32),
+            dma((n_bricks,)),
+            dma((GROUPS,)),
+            dma((2,)),
+        ],
+    )(brick_source, arrived, gram)
     return gram, tiles
 
 

time: 95.6 us -> 88.8 us (0.929)
  Pallas kernels: 93.5 us -> 87.4 us
    pallas_call x1, Pallas kernels: 89.8 us -> 83.5 us  [per_device(): pl.pallas_call(functools.partial(folded_kernel if folded else kernel, n_r...]
where the time goes in v3:
time: 88.8 us; the launch traced here: 88 us
  Pallas kernels  87.4 us (98%)
    pallas_call x1, Pallas kernels, per_device(): pl.pallas_call(functools.partial(folded_kernel if folded else kernel, n_r...  83.5 us
    pallas_call x1, Pallas kernels, per_device(): pl.pallas_call(functools.partial(place_bricks, n_bricks), out_shape=(jax....  3.86 us

profile of v3, /device:TPU:6, one launch (start us, length us, event | category | flops | bytes accessed | tf_op | source)
XLA Modules:
  0.0 88.0 jit_solution(10796351256372771520)
XLA Ops:
  0.6 83.5 %shard_map.59 = (f32[512,256]{1,0:T(8,128)}, f32[2048,256]{1,0:T(8,128)}) custom-call(f32[2048,256]{1,0:T(8,128)} %snap_in.1, f32[16,128]{1,0:T(8,128)} %bitcast.1, f32[256,2048]{1,0:T(8,128)} %bricks.1), custom_call_target="tpu_custom_call" | custom-call | tf_op jit(solution)/shard_map/pallas_call | solution.py:606
  84.2 3.9 %shard_map.60 = (f32[2048,256]{1,0:T(8,128)}, f32[512,256]{1,0:T(8,128)}) custom-call(s32[1,64]{1,0:T(1,128)} %order.1, f32[2048,256]{1,0:T(8,128)} %get-tuple-element.6.src, f32[512,256]{1,0:T(8,128)} %get-tuple-element.7.gram), custom_call_target="tpu_custom_call" | custom-call | tf_op jit(solution)/shard_map/pallas_call | solution.py:620

commit v4 on v3

--- a/solution.py
+++ b/solution.py
@@ -282,7 +282,7 @@
         )
 
     def brick_copy(k):
-        to = (s + k) % n_s
+        to = chip_at((t + k // 2) % n) * 2 + (c + k) % 2
         return pltpu.make_async_remote_copy(
             src_ref=bricks.at[:, pl.ds(pl.multiple_of(to * width, width), width)],
             dst_ref=arrived.at[pl.ds(pl.multiple_of(s * per_brick_dev, per_brick_dev), per_brick_dev)],
@@ -367,6 +367,7 @@
         own_sem.at[0],
     )
     own_bricks.start()
+    brick_copy(1).start()
     to_mate = pltpu.make_async_remote_copy(
         src_ref=snap, dst_ref=mate, send_sem=d_send.at[0], recv_sem=d_recv.at[0],
         device_id=(z, partner), device_id_type=MESH,
@@ -453,15 +454,13 @@
         ring_copy(first, stage).wait_send()
         ring_copy(second, stage).start()
     near(first)
-    reduce_quadrant(0)
     for stage in range(2):
         ring_copy(second, stage).wait_send()
         if stage == 0:
             ring_copy(first, 2).start()
     ring_copy(second, 0).wait_recv()
     ring_copy(second, 2).start()
-    for k in range(1, n_s):
-        brick_copy(k).start()
+    reduce_quadrant(0)
     ring_copy(second, 1).wait_recv()
     for stage in range(2):
         take(slot_of(second), start_of(second, owner_of(second), stage))
@@ -470,10 +469,14 @@
         ring_copy(way, 2).wait_recv()
         take(2, start_of(way, (t + 2) % n, 0))
     sides(2, lambda copy: copy.start())
+    for k in (4, 5):
+        brick_copy(k).start()
 
     order = (1, 3, 2)
     for d in order:
         reduce_quadrant(d)
+    for k in (2, 3, 6, 7):
+        brick_copy(k).start()
     for d in order:
         @pl.when(holds(d))
         def _():

time: 88.8 us -> 88.2 us (level)
  no operation moved by 1% of the time
where the time goes in v4:
time: 88.2 us; the launch traced here: 87.9 us
  Pallas kernels  87.3 us (99%)
    pallas_call x1, Pallas kernels, per_device(): pl.pallas_call(functools.partial(folded_kernel if folded else kernel, n_r...  83.4 us
    pallas_call x1, Pallas kernels, per_device(): pl.pallas_call(functools.partial(place_bricks, n_bricks), out_shape=(jax....  3.86 us

profile of v4, /device:TPU:6, one launch (start us, length us, event | category | flops | bytes accessed | tf_op | source)
XLA Modules:
  0.0 87.9 jit_solution(10055583494786430947)
XLA Ops:
  0.6 83.4 %shard_map.59 = (f32[512,256]{1,0:T(8,128)}, f32[2048,256]{1,0:T(8,128)}) custom-call(f32[2048,256]{1,0:T(8,128)} %snap_in.1, f32[16,128]{1,0:T(8,128)} %bitcast.1, f32[256,2048]{1,0:T(8,128)} %bricks.1), custom_call_target="tpu_custom_call" | custom-call | tf_op jit(solution)/shard_map/pallas_call | solution.py:609
  84.1 3.9 %shard_map.60 = (f32[2048,256]{1,0:T(8,128)}, f32[512,256]{1,0:T(8,128)}) custom-call(s32[1,64]{1,0:T(1,128)} %order.1, f32[2048,256]{1,0:T(8,128)} %get-tuple-element.6.src, f32[512,256]{1,0:T(8,128)} %get-tuple-element.7.gram), custom_call_target="tpu_custom_call" | custom-call | tf_op jit(solution)/shard_map/pallas_call | solution.py:623
